TPU v7x, 256 devices: a whole 4x4x8 slice. The times are simulated.
256 devices in a mesh: expert: 8 (over z), tp: 32 (over x, y, core).
Axes of the slice: x: 4, y: 4, z: 8, core: 2. Of those that a mesh axis runs over, the one named last changes fastest.
Arguments:
- tokens: bfloat16 [1024, 4096], P('expert', 'tp'), may hold values from -6 to 6
- norm_gain: bfloat16 [4096], replicated, may hold values from 0.5 to 1.5
- route_logits: float32 [1024, 2], P('expert'), may hold values from -6 to 6
- expert_ids: int32 [1024, 2], P('expert'), may hold values from 0 to 7, all different within a row; in each aligned block of 128 rows (0 to 127, 128 to 255, ...) at most 64 rows name the same one
- active: int32 [1024], P('expert'), may hold values 0 or 1
- gate_weight: bfloat16 [8, 14336, 4096], P('expert', 'tp'), may hold values from -0.09375 to 0.09375
- up_weight: bfloat16 [8, 14336, 4096], P('expert', 'tp'), may hold values from -0.09375 to 0.09375
- down_weight: bfloat16 [8, 14336, 4096], P('expert', 'tp'), may hold values from -0.046875 to 0.046875
Outputs:
- mixed: bfloat16 [1024, 4096], P('expert', 'tp')
Inputs may be any that keep to these rules, and one draw needn't show every extreme that they name: `expert_ids`: each token names 2 different experts. In each block of 128 consecutive token slots (the slots of one index of expert) no expert is named by more than 64 tokens, a bound that some block reaches. `active`: each entry is 0 or 1.
All inputs are finite; a program needn't handle non-finite values.
Results may differ from a plain program's by a relative error of at most 0.0025.
Values may be sent and summed in bfloat16 or wider, within the bound.
A program may use at most 64 MiB of HBM per device.

v0:
```python
import jax
import jax.numpy as jnp
from jax import lax
from jax.sharding import Mesh
from jax.sharding import PartitionSpec as P

TP = ("tp_0", "tp_1", "tp_2")
epsilon = 1e-05


def one_axis_at_a_time(shard, axes):
    for axis in axes:
        shard = lax.psum(shard, axis)
    return shard


def taken_in(shard, axis, dim, absorb, state):
    everything = jax.tree.map(lambda a: lax.all_gather(a, axis, axis=dim, tiled=True), shard)
    return absorb(state, everything, jnp.int32(0))


def own_rows(product, width, axis):
    everything = product(jnp.int32(0), lax.axis_size(axis) * width)
    own = lax.psum_scatter(everything, axis, scatter_dimension=0, tiled=True)
    return own


def slot_numbers(expert_ids, active, seat_limit, experts):
    flat_ids = expert_ids.reshape(-1)
    is_live = jnp.broadcast_to(active[:, None], expert_ids.shape).reshape(-1)
    columns = jnp.arange(experts, dtype=jnp.int32)
    one_hot = (flat_ids[:, None] == columns[None, :]).astype(jnp.int32) * is_live[:, None]
    earlier = jnp.cumsum(one_hot, axis=0) - one_hot
    position = jnp.sum(earlier * one_hot, axis=1)
    slot_index = jnp.where(is_live > 0, flat_ids * seat_limit + position, -1)
    return slot_index.reshape(expert_ids.shape)


def local(tokens, norm_gain, route_logits, expert_ids, active, gate_weight, up_weight, down_weight):
    expert_count = lax.axis_size("expert")
    tp_index = lax.axis_index(TP)
    token_count, feature_share = tokens.shape
    local_count, ff_share, model_width = gate_weight.shape
    seat_limit = token_count // 2
    experts = expert_count * local_count
    slots = expert_count * seat_limit
    gains = norm_gain.astype(jnp.float32)
    widened = tokens.astype(jnp.float32)
    squares = one_axis_at_a_time(jnp.sum(widened * widened, axis=1), TP)
    gain_part = lax.dynamic_slice_in_dim(gains, tp_index * feature_share, feature_share)
    mean_square = squares[:, None] / model_width
    normed = (widened * lax.rsqrt(mean_square + epsilon) * gain_part).astype(jnp.bfloat16)
    route_probs = jax.nn.softmax(route_logits, axis=1) * active.astype(jnp.float32)[:, None]
    slot_index = slot_numbers(expert_ids, active, seat_limit, experts)
    buffer_rows = experts * seat_limit
    targets = jnp.arange(buffer_rows, dtype=jnp.int32)
    pick_hot = (slot_index[:, :, None] == targets[None, None, :]).astype(jnp.bfloat16)
    send_hot = jnp.sum(pick_hot, axis=1)
    send_rows = jnp.einsum(
        "jr,jw->rw", send_hot, normed, preferred_element_type=jnp.float32
    ).astype(jnp.bfloat16)
    arriving = lax.all_to_all(send_rows, "expert", split_axis=0, concat_axis=0, tiled=True)
    received = arriving.reshape(expert_count, local_count, seat_limit, -1).transpose(1, 0, 2, 3)
    received = received.reshape(local_count, slots, -1)
    empty = jnp.zeros((local_count, slots, ff_share), jnp.float32)

    def add_projections(running, shard_piece, offset):
        sequence_extent = shard_piece.shape[2]
        gate_part = lax.dynamic_slice_in_dim(gate_weight, offset, sequence_extent, 2)
        up_part = lax.dynamic_slice_in_dim(up_weight, offset, sequence_extent, 2)
        gate_next = running[0] + jnp.einsum(
            "lrd,lfd->lrf", shard_piece, gate_part, preferred_element_type=jnp.float32
        )
        up_next = running[1] + jnp.einsum(
            "lrd,lfd->lrf", shard_piece, up_part, preferred_element_type=jnp.float32
        )
        return (gate_next, up_next)

    gate_sum, up_sum = taken_in(received, TP, 2, add_projections, (empty, empty))
    inner_width = (jax.nn.silu(gate_sum) * up_sum).astype(jnp.bfloat16)

    def down_terms(offset, count):
        lowering_share = lax.dynamic_slice_in_dim(down_weight, offset, count, 2)
        return jnp.einsum(
            "hzj,hjs->shz", inner_width, lowering_share, preferred_element_type=jnp.float32
        )

    reduced = own_rows(down_terms, feature_share, TP)
    specialist_result = reduced.transpose(1, 2, 0).astype(jnp.bfloat16)
    returning = specialist_result.reshape(
        local_count, expert_count, seat_limit, feature_share
    ).transpose(1, 0, 2, 3)
    returning = returning.reshape(expert_count * local_count * seat_limit, feature_share)
    arrived = lax.all_to_all(returning, "expert", split_axis=0, concat_axis=0, tiled=True)
    picked = jnp.einsum("jkr,rw->jkw", pick_hot, arrived, preferred_element_type=jnp.float32)
    mixed = jnp.sum(route_probs[:, :, None] * picked, axis=1)
    return mixed.astype(jnp.bfloat16)


def solution(mesh):
    split = Mesh(
        mesh.devices.reshape(mesh.shape["expert"], 4, 4, 2), ("expert", "tp_0", "tp_1", "tp_2")
    )
    in_specs = (
        P("expert", TP),
        P(),
        P("expert", None),
        P("expert", None),
        P("expert"),
        P("expert", TP, None),
        P("expert", TP, None),
        P("expert", TP, None),
    )
    out_specs = P("expert", TP)
    return jax.shard_map(local, mesh=split, in_specs=in_specs, out_specs=out_specs, check_vma=False)
```

profile of v0, /device:TPU:2, one launch (start us, length us, event | category | flops | bytes accessed | tf_op | source)
XLA Modules:
  0.0 244.5 jit_solution(12486279213063765660)
XLA Ops:
  6.5 0.0 all-gather.2.cloned.1.call-start
  6.5 0.8 copy.19
  7.3 0.1 eq.38
  7.5 0.1 eq.42
  7.6 0.7 broadcast_in_dim.27
  8.3 0.7 broadcast_compare_fusion
  9.0 0.1 broadcast_in_dim.28
  9.1 0.1 broadcast_in_dim.29
  9.2 0.6 reduce-window.6
  9.8 0.2 slice_reduce_fusion
  10.1 0.7 broadcast_in_dim.30
  10.8 0.1 mul.85
  11.0 0.1 fusion.36
  11.1 0.1 reduce_sum.52
  11.2 0.1 copy.21
  11.3 0.7 add_select_fusion
  12.0 0.1 fusion.28
  12.1 0.9 fusion.30
  13.0 10.0 %psum.21 = f32[128]{0:T(128)S(1)} all-reduce(f32[128]{0:T(128)S(1)} %fusion.30), channel_id=1, replica_groups=mesh['expert'=8,'tp_0'=4,'tp_1'=4,'tp_2'=2] {'tp_0'}, use_global_device_ids=true, to_apply=%region_7.8 | all-reduce | flops 128 | bytes 1024 | tf_op jit(solution)/shard_map/psum | solution.py:13
  22.9 9.4 %psum.22 = f32[128]{0:T(128)S(1)} all-reduce(f32[128]{0:T(128)S(1)} %psum.21), channel_id=1, replica_groups=mesh['expert'=8,'tp_0'=4,'tp_1'=4,'tp_2'=2] {'tp_1'}, use_global_device_ids=true, to_apply=%region_8.9 | all-reduce | flops 128 | bytes 1024 | tf_op jit(solution)/shard_map/psum | solution.py:13
  32.3 2.5 %psum.23 = f32[128]{0:T(128)S(1)} all-reduce(f32[128]{0:T(128)S(1)} %psum.22), channel_id=1, replica_groups=mesh['expert'=8,'tp_0'=4,'tp_1'=4,'tp_2'=2] {'tp_2'}, use_global_device_ids=true, to_apply=%region_9.10 | all-reduce | flops 128 | bytes 1024 | tf_op jit(solution)/shard_map/psum | solution.py:13
  34.8 0.8 dynamic-slice_convert_fusion
  35.5 1.0 convolution_convert_fusion
  36.5 17.8 %all_to_all.21 = bf16[8,64,128]{2,1,0:T(8,128)(2,1)} all-to-all(bf16[8,64,128]{2,1,0:T(8,128)(2,1)S(1)} %bitcast.45), channel_id=1, replica_groups=mesh['expert'=8,'tp_0'=4,'tp_1'=4,'tp_2'=2] {'expert'}, dimensions={0} | all-to-all | bytes 262144 | tf_op jit(solution)/shard_map/all_to_all | solution.py:62
  54.3 0.0 all-gather.2.cloned.1.call-update
  54.3 0.0 reduce-scatter.2.cloned.1.call-start
  54.4 47.1 %all-gather.2.cloned.1.call-done = bf16[1,512,4096]{2,1,0:T(8,128)(2,1)} async-done(((bf16[1,512,128]{2,1,0:T(8,128)(2,1)}), bf16[1,512,4096]{2,1,0:T(8,128)(2,1)}) %all-gather.2.cloned.1.call-update) | async-done | bytes 4194320 | tf_op jit(solution)/shard_map/all_gather | solution.py:18
  101.5 5.4 %fusion.2 = f32[512,448]{0,1:T(8,128)S(1)} fusion(bf16[1,512,4096]{2,1,0:T(8,128)(2,1)} %all-gather.2.cloned.1.call-done, bf16[1,448,4096]{2,1,0:T(8,128)(2,1)} %param.13), kind=kOutput, calls=%fused_computation.3 | convolution fusion | flops 1879048192 | bytes 8781824 | tf_op jit(solution)/shard_map/lrd,lfd->lrf/dot_general | solution.py:71
  106.9 12.0 %convolution_bitcast_fusion = f32[4096,1,512]{0,2,1:T(8,128)} fusion(bf16[1,448,4096]{2,1,0:T(8,128)(2,1)} %param.15, bf16[1,448,4096]{2,1,0:T(8,128)(2,1)} %param.14, bf16[1,512,4096]{2,1,0:T(8,128)(2,1)} %all-gather.2.cloned.1.call-done, f32[512,448]{0,1:T(8,128)S(1)} %fusion.2), kind=kOutput, calls=%fused_computation | convolution fusion | flops 3759472640 | bytes 20840448 | tf_op jit(solution)/shard_map/hzj,hjs->shz/dot_general | solution.py:84
  118.9 0.0 copy-start
  118.9 0.0 copy-start.1
  118.9 0.0 reduce-scatter.2.cloned.1.call-update
  118.9 0.7 copy-done
  119.6 99.4 %reduce-scatter.2.cloned.1.call-done = f32[128,1,512]{0,2,1:T(8,128)} async-done(((f32[4096,1,512]{0,2,1:T(8,128)}), f32[128,1,512]{0,2,1:T(8,128)}) %reduce-scatter.2.cloned.1.call-update) | async-done | bytes 262160 | tf_op jit(solution)/shard_map/reduce_scatter | solution.py:24
  219.1 1.6 convert_element_type.41
  220.7 7.0 %all-to-all-start.1 = ((bf16[8,64,128]{2,1,0:T(8,128)(2,1)}), bf16[8,64,128]{2,1,0:T(8,128)(2,1)S(1)}, u32[]{:S(2)}, u32[]{:S(2)}) async-start(bf16[8,64,128]{2,1,0:T(8,128)(2,1)} %bitcast.11), calls=%async_computation.2 | async-start | bytes 262144 | tf_op jit(solution)/shard_map/all_to_all | solution.py:94
  227.7 0.0 copy-done.1
  227.7 9.0 %all-to-all-done.1 = bf16[8,64,128]{2,1,0:T(8,128)(2,1)S(1)} async-done(((bf16[8,64,128]{2,1,0:T(8,128)(2,1)}), bf16[8,64,128]{2,1,0:T(8,128)(2,1)S(1)}, u32[]{:S(2)}, u32[]{:S(2)}) %all-to-all-start.1) | async-done | bytes 131104 | tf_op jit(solution)/shard_map/all_to_all | solution.py:94
  236.7 0.9 fusion.17
  (8 shorter events, 0.1 us)
Async XLA Ops:
  6.5 94.9 %all-gather.2.cloned.1.call-start = ((), (), s32[]{:S(2)}) async-start(), calls=%async_computation.3 | async-start | bytes 4325376 | tf_op jit(solution)/shard_map/all_gather | solution.py:18
  54.3 164.7 %reduce-scatter.2.cloned.1.call-start = ((), (), s32[]{:S(2)}) async-start(), calls=%async_computation.4 | async-start | bytes 8650752 | tf_op jit(solution)/shard_map/reduce_scatter | solution.py:24
  118.9 0.7 copy-start
  118.9 108.8 %copy-start.1 = (s32[128]{0:T(128)S(1)}, s32[128]{0:T(128)}, u32[]{:S(2)}) copy-start(s32[128]{0:T(128)} %param.12) | copy-start | bytes 1540
  220.7 16.1 %all-to-all-start.1 = ((bf16[8,64,128]{2,1,0:T(8,128)(2,1)}), bf16[8,64,128]{2,1,0:T(8,128)(2,1)S(1)}, u32[]{:S(2)}, u32[]{:S(2)}) async-start(bf16[8,64,128]{2,1,0:T(8,128)(2,1)} %bitcast.11), calls=%async_computation.2 | async-start | bytes 262144 | tf_op jit(solution)/shard_map/all_to_all | solution.py:94
Sparse Core Ops, SparseCore 0:
  54.5 46.9 all-gather.1
  119.1 99.9 reduce-scatter.1
where the time goes:
time: 245 us; the launch traced here: 244 us
  waiting for transfers between devices  156 us (64%)
  blocking collectives  39.6 us (16%)
  matrix products  19.3 us (8%)
  between operations  13.5 us (6%)
  starting transfers between devices  7.05 us (3%)
  other arithmetic  5.48 us (2%)
  local copies, waits for them, and re-layouts  3.98 us (2%)
    reduce_scatter x1, waiting for transfers between devices, own_rows(): own = lax.psum_scatter(everything, axis, scatter_dimension=0, tiled=True)  99.4 us
    all_gather x1, waiting for transfers between devices, taken_in(): lax.all_gather(a, axis, axis=dim, tiled=True)  47.1 us
    psum x3, blocking collectives, one_axis_at_a_time(): shard = lax.psum(shard, axis)  21.8 us
    all_to_all x1, blocking collectives, local(): lax.all_to_all(send_rows, 'expert', split_axis=0, concat_axis=0, tiled=True)  17.8 us
    dot_general x1, matrix products, down_terms(): jnp.einsum('hzj,hjs->shz', inner_width, lowering_share, preferred_element...  12 us
    all_to_all x1, waiting for transfers between devices, local(): lax.all_to_all(returning, 'expert', split_axis=0, concat_axis=0, tiled=True)  9.03 us
    all_to_all x1, starting transfers between devices, local(): lax.all_to_all(returning, 'expert', split_axis=0, concat_axis=0, tiled=True)  7.01 us
    dot_general x1, matrix products, add_projections(): jnp.einsum('lrd,lfd->lrf', shard_piece, gate_part, preferred_element_type...  5.4 us
  transfers between devices with their start and end apart: 3, of which 3 were waited for; matrix products, arithmetic and copies ran while one was open for 0% of the time, Pallas kernels for 0%

commit v1 on v0

--- a/solution.py
+++ b/solution.py
@@ -6,6 +6,32 @@
 
 TP = ("tp_0", "tp_1", "tp_2")
 epsilon = 1e-05
+
+
+def boxes_build(here_x, in_dim, mat):
+    ready, y2 = (here_x.shape[:in_dim], here_x.shape[in_dim + 1 :])
+    return jnp.moveaxis(here_x.reshape(*ready, mat, -1, *y2), in_dim, 0)
+
+
+def take_seats_all_for(block_in, dim_k):
+    block_in = jnp.moveaxis(block_in, 0, dim_k)
+    work_now = block_in.shape
+    return block_in.reshape(
+        *work_now[:dim_k], work_now[dim_k] * work_now[dim_k + 1], *work_now[dim_k + 2 :]
+    )
+
+
+def state_point_over_axis(target, axis_name, vec, m):
+    r1, side_arr = (lax.axis_size(axis_name), lax.axis_index(axis_name))
+    prior = boxes_build(target, vec, r1)
+    shelf = [prior[side_arr]]
+    no = 1
+    while no < r1:
+        out_arr = prior[side_arr ^ no]
+        shelf.append(lax.ppermute(out_arr, axis_name, perm=[(b, b ^ no) for b in range(r1)]))
+        no = no + 1
+    prior = jnp.stack(shelf)[side_arr ^ jnp.arange(r1)]
+    return take_seats_all_for(prior, m)
 
 
 def one_axis_at_a_time(shard, axes):
@@ -59,7 +85,7 @@
     send_rows = jnp.einsum(
         "jr,jw->rw", send_hot, normed, preferred_element_type=jnp.float32
     ).astype(jnp.bfloat16)
-    arriving = lax.all_to_all(send_rows, "expert", split_axis=0, concat_axis=0, tiled=True)
+    arriving = state_point_over_axis(send_rows, "expert", 0, 0)
     received = arriving.reshape(expert_count, local_count, seat_limit, -1).transpose(1, 0, 2, 3)
     received = received.reshape(local_count, slots, -1)
     empty = jnp.zeros((local_count, slots, ff_share), jnp.float32)

time: 245 us -> 252 us (1.029)
  blocking collectives: 39.6 us -> 21.8 us
  starting transfers between devices: 7.05 us -> 23.4 us
  waiting for transfers between devices: 156 us -> 162 us
    all_to_all x1 -> x0, blocking collectives: 17.8 us -> none  [local(): lax.all_to_all(send_rows, 'expert', split_axis=0, concat_axis=0, tiled=True)]
    ppermute x0 -> x7, starting transfers between devices: none -> 16.4 us  [state_point_over_axis(): lax.ppermute(out_arr, axis_name, perm=[(b, b ^ no) for b in range(r1)])]
    ppermute x0 -> x7, waiting for transfers between devices: none -> 4.88 us  [state_point_over_axis(): lax.ppermute(out_arr, axis_name, perm=[(b, b ^ no) for b in range(r1)])]
  transfers between devices with their start and end apart: 3 -> 10, of which waited for: 3 -> 5; matrix products, arithmetic and copies ran while one was open for 0% -> 0% of each run, Pallas kernels for 0% -> 0%
where the time goes in v1:
time: 252 us; the launch traced here: 251 us
  waiting for transfers between devices  162 us (64%)
  starting transfers between devices  23.4 us (9%)
  blocking collectives  21.8 us (9%)
  matrix products  19.3 us (8%)
  between operations  13.5 us (5%)
  other arithmetic  5.5 us (2%)
  local copies, waits for them, and re-layouts  5.27 us (2%)
    reduce_scatter x1, waiting for transfers between devices, own_rows(): own = lax.psum_scatter(everything, axis, scatter_dimension=0, tiled=True)  99.4 us
    all_gather x1, waiting for transfers between devices, taken_in(): lax.all_gather(a, axis, axis=dim, tiled=True)  48.9 us
    psum x3, blocking collectives, one_axis_at_a_time(): shard = lax.psum(shard, axis)  21.8 us
    ppermute x7, starting transfers between devices, state_point_over_axis(): lax.ppermute(out_arr, axis_name, perm=[(b, b ^ no) for b in range(r1)])  16.4 us
    dot_general x1, matrix products, down_terms(): jnp.einsum('hzj,hjs->shz', inner_width, lowering_share, preferred_element...  12 us
    all_to_all x1, waiting for transfers between devices, local(): lax.all_to_all(returning, 'expert', split_axis=0, concat_axis=0, tiled=True)  9.03 us
    all_to_all x1, starting transfers between devices, local(): lax.all_to_all(returning, 'expert', split_axis=0, concat_axis=0, tiled=True)  7.04 us
    dot_general x1, matrix products, add_projections(): jnp.einsum('lrd,lfd->lrf', shard_piece, gate_part, preferred_element_type...  5.4 us
  transfers between devices with their start and end apart: 10, of which 5 were waited for; matrix products, arithmetic and copies ran while one was open for 0% of the time, Pallas kernels for 0%

profile of v1, /device:TPU:2, one launch (start us, length us, event | category | flops | bytes accessed | tf_op | source)
XLA Modules:
  0.0 251.1 jit_solution(11042070014529382971)
XLA Ops:
  6.5 0.0 all-gather.2.cloned.1.call-start
  6.5 0.8 copy.19
  7.3 0.1 eq.38
  7.5 0.1 eq.42
  7.6 0.7 broadcast_in_dim.28
  8.3 0.7 broadcast_compare_fusion
  9.0 0.1 broadcast_in_dim.29
  9.1 0.1 broadcast_in_dim.30
  9.2 0.6 reduce-window.6
  9.8 0.2 slice_reduce_fusion
  10.1 0.7 broadcast_in_dim.31
  10.8 0.1 mul.85
  11.0 0.1 fusion.36
  11.1 0.1 reduce_sum.52
  11.2 0.1 copy.21
  11.3 0.7 add_select_fusion
  12.0 0.1 fusion.28
  12.1 0.9 fusion.30
  13.0 10.0 %psum.21 = f32[128]{0:T(128)S(1)} all-reduce(f32[128]{0:T(128)S(1)} %fusion.30), channel_id=1, replica_groups=mesh['expert'=8,'tp_0'=4,'tp_1'=4,'tp_2'=2] {'tp_0'}, use_global_device_ids=true, to_apply=%region_7.8 | all-reduce | flops 128 | bytes 1024 | tf_op jit(solution)/shard_map/psum | solution.py:39
  22.9 9.4 %psum.22 = f32[128]{0:T(128)S(1)} all-reduce(f32[128]{0:T(128)S(1)} %psum.21), channel_id=1, replica_groups=mesh['expert'=8,'tp_0'=4,'tp_1'=4,'tp_2'=2] {'tp_1'}, use_global_device_ids=true, to_apply=%region_8.9 | all-reduce | flops 128 | bytes 1024 | tf_op jit(solution)/shard_map/psum | solution.py:39
  32.3 2.5 psum.23
  34.8 0.8 dynamic-slice_convert_fusion
  35.5 1.0 convolution_convert_fusion
  36.6 2.0 collective-permute-start
  38.6 3.3 %collective-permute-start.1 = (bf16[64,128]{1,0:T(8,128)(2,1)S(1)}, bf16[64,128]{1,0:T(8,128)(2,1)S(1)}, u32[]{:S(2)}, u32[]{:S(2)}) collective-permute-start(bf16[64,128]{1,0:T(8,128)(2,1)S(1)} %get-tuple-element.10), channel_id=1, source_target_pairs={{0,64},{32,96},{64,0},{96,32},{128,192},{160,224},{192,128},{224,1... | collective-permute-start | bytes 49160 | tf_op jit(solution)/shard_map/ppermute | solution.py:31
  41.9 0.0 collective-permute-start.2
  41.9 6.4 %collective-permute-start.3 = (bf16[64,128]{1,0:T(8,128)(2,1)S(1)}, bf16[64,128]{1,0:T(8,128)(2,1)S(1)}, u32[]{:S(2)}, u32[]{:S(2)}) collective-permute-start(bf16[64,128]{1,0:T(8,128)(2,1)S(1)} %get-tuple-element.8), channel_id=1, source_target_pairs={{0,128},{32,160},{64,192},{96,224},{128,0},{160,32},{192,64},{224,... | collective-permute-start | bytes 49160 | tf_op jit(solution)/shard_map/ppermute | solution.py:31
  48.2 0.0 collective-permute-start.4
  48.3 0.0 collective-permute-done
  48.3 4.7 %collective-permute-start.5 = (bf16[64,128]{1,0:T(8,128)(2,1)S(1)}, bf16[64,128]{1,0:T(8,128)(2,1)S(1)}, u32[]{:S(2)}, u32[]{:S(2)}) collective-permute-start(bf16[64,128]{1,0:T(8,128)(2,1)S(1)} %get-tuple-element.6), channel_id=1, source_target_pairs={{0,192},{32,224},{64,128},{96,160},{128,64},{160,96},{192,0},{224,... | collective-permute-start | bytes 49160 | tf_op jit(solution)/shard_map/ppermute | solution.py:31
  53.0 0.0 collective-permute-done.1
  53.0 0.0 collective-permute-start.6
  53.0 0.0 collective-permute-done.2
  53.0 0.0 collective-permute-done.3
  53.0 2.0 collective-permute-done.4
  55.0 0.0 collective-permute-done.5
  55.0 2.9 %collective-permute-done.6 = bf16[64,128]{1,0:T(8,128)(2,1)S(1)} collective-permute-done((bf16[64,128]{1,0:T(8,128)(2,1)S(1)}, bf16[64,128]{1,0:T(8,128)(2,1)S(1)}, u32[]{:S(2)}, u32[]{:S(2)}) %collective-permute-start.6) | collective-permute-done | bytes 16416 | tf_op jit(solution)/shard_map/ppermute | solution.py:31
  57.9 1.2 gather_fusion
  59.1 0.0 all-gather.2.cloned.1.call-update
  59.1 0.0 reduce-scatter.2.cloned.1.call-start
  59.2 48.9 %all-gather.2.cloned.1.call-done = bf16[1,512,4096]{2,1,0:T(8,128)(2,1)} async-done(((bf16[1,512,128]{2,1,0:T(8,128)(2,1)}), bf16[1,512,4096]{2,1,0:T(8,128)(2,1)}) %all-gather.2.cloned.1.call-update) | async-done | bytes 4194320 | tf_op jit(solution)/shard_map/all_gather | solution.py:44
  108.1 5.4 %fusion.2 = f32[512,448]{0,1:T(8,128)S(1)} fusion(bf16[1,512,4096]{2,1,0:T(8,128)(2,1)} %all-gather.2.cloned.1.call-done, bf16[1,448,4096]{2,1,0:T(8,128)(2,1)} %param.13), kind=kOutput, calls=%fused_computation.4 | convolution fusion | flops 1879048192 | bytes 8781824 | tf_op jit(solution)/shard_map/lrd,lfd->lrf/dot_general | solution.py:97
  113.5 12.0 %convolution_bitcast_fusion = f32[4096,1,512]{0,2,1:T(8,128)} fusion(bf16[1,448,4096]{2,1,0:T(8,128)(2,1)} %param.15, bf16[1,448,4096]{2,1,0:T(8,128)(2,1)} %param.14, bf16[1,512,4096]{2,1,0:T(8,128)(2,1)} %all-gather.2.cloned.1.call-done, f32[512,448]{0,1:T(8,128)S(1)} %fusion.2), kind=kOutput, calls=%fused_computation.1 | convolution fusion | flops 3759472640 | bytes 20840448 | tf_op jit(solution)/shard_map/hzj,hjs->shz/dot_general | solution.py:110
  125.5 0.0 copy-start
  125.5 0.0 copy-start.1
  125.5 0.0 reduce-scatter.2.cloned.1.call-update
  125.5 0.7 copy-done
  126.2 99.4 %reduce-scatter.2.cloned.1.call-done = f32[128,1,512]{0,2,1:T(8,128)} async-done(((f32[4096,1,512]{0,2,1:T(8,128)}), f32[128,1,512]{0,2,1:T(8,128)}) %reduce-scatter.2.cloned.1.call-update) | async-done | bytes 262160 | tf_op jit(solution)/shard_map/reduce_scatter | solution.py:50
  225.6 1.6 convert_element_type.41
  227.2 7.0 %all-to-all-start = ((bf16[8,64,128]{2,1,0:T(8,128)(2,1)}), bf16[8,64,128]{2,1,0:T(8,128)(2,1)S(1)}, u32[]{:S(2)}, u32[]{:S(2)}) async-start(bf16[8,64,128]{2,1,0:T(8,128)(2,1)} %bitcast.26), calls=%async_computation.1 | async-start | bytes 262144 | tf_op jit(solution)/shard_map/all_to_all | solution.py:120
  234.3 0.0 copy-done.1
  234.3 9.0 %all-to-all-done = bf16[8,64,128]{2,1,0:T(8,128)(2,1)S(1)} async-done(((bf16[8,64,128]{2,1,0:T(8,128)(2,1)}), bf16[8,64,128]{2,1,0:T(8,128)(2,1)S(1)}, u32[]{:S(2)}, u32[]{:S(2)}) %all-to-all-start) | async-done | bytes 131104 | tf_op jit(solution)/shard_map/all_to_all | solution.py:120
  243.3 0.9 fusion.17
  (18 shorter events, 0.2 us)
Async XLA Ops:
  6.5 101.5 %all-gather.2.cloned.1.call-start = ((), (), s32[]{:S(2)}) async-start(), calls=%async_computation.2 | async-start | bytes 4325376 | tf_op jit(solution)/shard_map/all_gather | solution.py:44
  36.6 11.7 %collective-permute-start = (bf16[64,128]{1,0:T(8,128)(2,1)S(1)}, bf16[64,128]{1,0:T(8,128)(2,1)S(1)}, u32[]{:S(2)}, u32[]{:S(2)}) collective-permute-start(bf16[64,128]{1,0:T(8,128)(2,1)S(1)} %get-tuple-element.11), channel_id=1, source_target_pairs={{0,32},{32,0},{64,96},{96,64},{128,160},{160,128},{192,224},{224,1... | collective-permute-start | bytes 49160 | tf_op jit(solution)/shard_map/ppermute | solution.py:31
  38.6 14.4 %collective-permute-start.1 = (bf16[64,128]{1,0:T(8,128)(2,1)S(1)}, bf16[64,128]{1,0:T(8,128)(2,1)S(1)}, u32[]{:S(2)}, u32[]{:S(2)}) collective-permute-start(bf16[64,128]{1,0:T(8,128)(2,1)S(1)} %get-tuple-element.10), channel_id=1, source_target_pairs={{0,64},{32,96},{64,0},{96,32},{128,192},{160,224},{192,128},{224,1... | collective-permute-start | bytes 49160 | tf_op jit(solution)/shard_map/ppermute | solution.py:31
  41.9 11.1 %collective-permute-start.2 = (bf16[64,128]{1,0:T(8,128)(2,1)S(1)}, bf16[64,128]{1,0:T(8,128)(2,1)S(1)}, u32[]{:S(2)}, u32[]{:S(2)}) collective-permute-start(bf16[64,128]{1,0:T(8,128)(2,1)S(1)} %get-tuple-element.9), channel_id=1, source_target_pairs={{0,96},{32,64},{64,32},{96,0},{128,224},{160,192},{192,160},{224,1... | collective-permute-start | bytes 49160 | tf_op jit(solution)/shard_map/ppermute | solution.py:31
  41.9 11.2 %collective-permute-start.3 = (bf16[64,128]{1,0:T(8,128)(2,1)S(1)}, bf16[64,128]{1,0:T(8,128)(2,1)S(1)}, u32[]{:S(2)}, u32[]{:S(2)}) collective-permute-start(bf16[64,128]{1,0:T(8,128)(2,1)S(1)} %get-tuple-element.8), channel_id=1, source_target_pairs={{0,128},{32,160},{64,192},{96,224},{128,0},{160,32},{192,64},{224,... | collective-permute-start | bytes 49160 | tf_op jit(solution)/shard_map/ppermute | solution.py:31
  48.2 6.7 %collective-permute-start.4 = (bf16[64,128]{1,0:T(8,128)(2,1)S(1)}, bf16[64,128]{1,0:T(8,128)(2,1)S(1)}, u32[]{:S(2)}, u32[]{:S(2)}) collective-permute-start(bf16[64,128]{1,0:T(8,128)(2,1)S(1)} %get-tuple-element.7), channel_id=1, source_target_pairs={{0,160},{32,128},{64,224},{96,192},{128,32},{160,0},{192,96},{224,... | collective-permute-start | bytes 49160 | tf_op jit(solution)/shard_map/ppermute | solution.py:31
  48.3 6.7 %collective-permute-start.5 = (bf16[64,128]{1,0:T(8,128)(2,1)S(1)}, bf16[64,128]{1,0:T(8,128)(2,1)S(1)}, u32[]{:S(2)}, u32[]{:S(2)}) collective-permute-start(bf16[64,128]{1,0:T(8,128)(2,1)S(1)} %get-tuple-element.6), channel_id=1, source_target_pairs={{0,192},{32,224},{64,128},{96,160},{128,64},{160,96},{192,0},{224,... | collective-permute-start | bytes 49160 | tf_op jit(solution)/shard_map/ppermute | solution.py:31
  53.0 5.0 %collective-permute-start.6 = (bf16[64,128]{1,0:T(8,128)(2,1)S(1)}, bf16[64,128]{1,0:T(8,128)(2,1)S(1)}, u32[]{:S(2)}, u32[]{:S(2)}) collective-permute-start(bf16[64,128]{1,0:T(8,128)(2,1)S(1)} %get-tuple-element.5), channel_id=1, source_target_pairs={{0,224},{32,192},{64,160},{96,128},{128,96},{160,64},{192,32},{224... | collective-permute-start | bytes 49160 | tf_op jit(solution)/shard_map/ppermute | solution.py:31
  59.1 166.5 %reduce-scatter.2.cloned.1.call-start = ((), (), s32[]{:S(2)}) async-start(), calls=%async_computation.3 | async-start | bytes 8650752 | tf_op jit(solution)/shard_map/reduce_scatter | solution.py:50
  125.5 0.7 copy-start
  125.5 108.8 %copy-start.1 = (s32[128]{0:T(128)S(1)}, s32[128]{0:T(128)}, u32[]{:S(2)}) copy-start(s32[128]{0:T(128)} %param.12) | copy-start | bytes 1540
  227.2 16.1 %all-to-all-start = ((bf16[8,64,128]{2,1,0:T(8,128)(2,1)}), bf16[8,64,128]{2,1,0:T(8,128)(2,1)S(1)}, u32[]{:S(2)}, u32[]{:S(2)}) async-start(bf16[8,64,128]{2,1,0:T(8,128)(2,1)} %bitcast.26), calls=%async_computation.1 | async-start | bytes 262144 | tf_op jit(solution)/shard_map/all_to_all | solution.py:120
Sparse Core Ops, SparseCore 0:
  59.3 48.7 all-gather.1
  125.7 99.9 reduce-scatter.1
